TPU v7x, 1024 devices: a whole 4x4x32 slice. The times are simulated.
1024 devices in a mesh: expert: 64 (over z_lo, x), replica: 16 (over z_hi, y, core).
Axes of the slice: x: 4, y: 4, z: 32 (z_hi: 2, z_lo: 16; z = z_hi * 16 + z_lo), core: 2. Of those that a mesh axis runs over, the one named last changes fastest.
Arguments:
- a_tokens: bfloat16 [65536, 2048], P(('expert', 'replica')), may hold values from -6 to 6
- a_ids: int32 [65536, 6], P(('expert', 'replica')), may hold values from 0 to 63, all different within a row
- a_gates: float32 [65536, 6], P(('expert', 'replica')), may hold values from 0.05 to 0.6
- a_valid: int32 [65536], P(('expert', 'replica')), may hold values 0 or 1
- b_cot: bfloat16 [65536, 2048], P(('expert', 'replica')), may hold values from -1.25 to 1.25
- b_ids: int32 [65536, 6], P(('expert', 'replica')), may hold values from 0 to 63, all different within a row
- b_gates: float32 [65536, 6], P(('expert', 'replica')), may hold values from 0.05 to 0.6
- b_valid: int32 [65536], P(('expert', 'replica')), may hold values 0 or 1
- b_hidden: bfloat16 [64, 6144, 704], P('expert', 'replica'), may hold values from -6 to 6
- w_gate: bfloat16 [64, 2048, 704], P('expert'), may hold values from -0.125 to 0.125
- w_up: bfloat16 [64, 2048, 704], P('expert'), may hold values from -0.125 to 0.125
- w_down: bfloat16 [64, 704, 2048], P('expert'), may hold values from -0.21875 to 0.21875
Outputs:
- a_out: bfloat16 [65536, 2048], P(('expert', 'replica'))
- grad_down: float32 [64, 704, 2048], P('expert', None, 'replica')
Inputs may be any that keep to these rules, and one draw needn't show every extreme that they name: `a_ids`: each token names 6 different experts. `b_ids`: each token names 6 different experts.
All inputs are finite; a program needn't handle non-finite values. No bound on the sum of `a_valid` or of `b_valid` on one device may be relied on, other than what follows from the above.
Results may differ from a plain program's by a relative error of at most 0.012.
Values may be sent and summed in bfloat16 or wider, within the bound.
A program may use at most 64 MiB of HBM per device.

v0:
```python
import jax
import jax.numpy as jnp
from jax import lax
from jax.sharding import PartitionSpec as P


def slot_keys(expert_ids, valid_mask, experts, capacity):
    top_count = expert_ids.shape[1]
    flat_ids = expert_ids.reshape(-1)
    live = jnp.repeat(valid_mask, top_count) > 0
    onehot = (
        (flat_ids[:, None] == jnp.arange(experts, dtype=jnp.int32)[None, :]) & live[:, None]
    ).astype(jnp.int32)
    earlier = jnp.cumsum(onehot, axis=0) - onehot
    position = jnp.sum(earlier * onehot, axis=1)
    kept_mask = live & (position < capacity)
    return jnp.where(kept_mask, flat_ids * capacity + position, -1)


def gather_tokens(slot_key, tokens, experts, capacity):
    total = experts * capacity
    tok_count = tokens.shape[0]
    matches = jnp.arange(total, dtype=jnp.int32)[:, None] == slot_key[None, :]
    picker = jnp.any(matches.reshape(total, tok_count, -1), axis=2).astype(jnp.bfloat16)
    sent = jnp.dot(picker, tokens, preferred_element_type=jnp.float32).astype(jnp.bfloat16)
    return sent.reshape(experts, capacity, tokens.shape[1])


def gated_slots(slot_key, gate_values, cotangent, experts, capacity):
    total = experts * capacity
    tok_count = cotangent.shape[0]
    flat_gates = gate_values.reshape(-1)
    matches = jnp.arange(total, dtype=jnp.int32)[:, None] == slot_key[None, :]
    picker = jnp.any(matches.reshape(total, tok_count, -1), axis=2).astype(jnp.bfloat16)
    copied = jnp.dot(picker, cotangent, preferred_element_type=jnp.float32)
    slot_gate = jnp.sum(
        jnp.where(matches, flat_gates[None, :], jnp.zeros_like(flat_gates)[None, :]), axis=1
    )
    slots = copied * slot_gate[:, None]
    return slots.astype(jnp.bfloat16).reshape(experts, capacity, cotangent.shape[1])


def combine_slots(slot_key, gate_values, returned):
    model_width = returned.shape[-1]
    flat_rows = returned.reshape(-1, model_width)
    picked = flat_rows[jnp.maximum(slot_key, 0)]
    flat_gates = gate_values.reshape(-1)
    scale = jnp.where(slot_key >= 0, flat_gates, jnp.zeros_like(flat_gates))
    summed = picked.astype(flat_gates.dtype) * scale[:, None]
    return jnp.sum(
        summed.reshape(gate_values.shape[0], gate_values.shape[1], model_width), axis=1
    ).astype(jnp.bfloat16)


def expert_ffn(inputs, gate_weight, up_weight, down_weight):
    model_width = inputs.shape[-1]
    rows = inputs.reshape(-1, model_width)
    gate_proj = jnp.dot(rows, gate_weight, preferred_element_type=jnp.float32)
    up_proj = jnp.dot(rows, up_weight, preferred_element_type=jnp.float32)
    hidden = (jax.nn.silu(gate_proj) * up_proj).astype(jnp.bfloat16)
    result = jnp.dot(hidden, down_weight, preferred_element_type=jnp.float32).astype(jnp.bfloat16)
    return result.reshape(inputs.shape[:-1] + (down_weight.shape[1],))


def body(
    a_tokens,
    a_ids,
    a_gates,
    a_valid,
    b_cot,
    b_ids,
    b_gates,
    b_valid,
    b_hidden,
    w_gate,
    w_up,
    w_down,
):
    experts = lax.axis_size("expert")
    capacity = b_hidden.shape[1] // experts
    model_width = a_tokens.shape[1]
    a_keys = slot_keys(a_ids, a_valid, experts, capacity)
    a_send = gather_tokens(a_keys, a_tokens, experts, capacity)
    b_keys = slot_keys(b_ids, b_valid, experts, capacity)
    b_send = gated_slots(b_keys, b_gates, b_cot, experts, capacity)
    produced = expert_ffn(
        lax.all_to_all(a_send, "expert", split_axis=0, concat_axis=0, tiled=True),
        w_gate[0],
        w_up[0],
        w_down[0],
    )
    a_back = lax.all_to_all(produced, "expert", split_axis=0, concat_axis=0, tiled=True)
    b_recv = lax.all_to_all(b_send, "expert", split_axis=0, concat_axis=0, tiled=True)
    a_out = combine_slots(a_keys, a_gates, a_back)
    partial_grad = jnp.dot(
        b_hidden[0].T, b_recv.reshape(-1, model_width), preferred_element_type=jnp.float32
    )
    gradient = lax.psum_scatter(
        partial_grad.astype(jnp.bfloat16), "replica", scatter_dimension=1, tiled=True
    ).astype(jnp.float32)
    return (a_out, gradient[None])


def solution(mesh):
    placed = (
        P(("expert", "replica"), None),
        P(("expert", "replica"), None),
        P(("expert", "replica"), None),
        P(("expert", "replica")),
        P(("expert", "replica"), None),
        P(("expert", "replica"), None),
        P(("expert", "replica"), None),
        P(("expert", "replica")),
        P("expert", "replica", None),
        P("expert", None, None),
        P("expert", None, None),
        P("expert", None, None),
    )
    return jax.shard_map(
        body,
        mesh=mesh,
        in_specs=placed,
        out_specs=(P(("expert", "replica"), None), P("expert", None, "replica")),
        check_vma=False,
    )
```

profile of v0, /device:TPU:2, one launch (start us, length us, event | category | flops | bytes accessed | tf_op | source)
XLA Modules:
  0.0 801.6 jit_solution(11277250854010418619)
XLA Ops:
  10.2 0.9 reduce-window.14
  12.0 2.7 convolution_convert_fusion.1
  14.7 3.7 reshape.206
  18.4 29.7 %all-to-all-start = ((bf16[64,6,2048]{2,1,0:T(8,128)(2,1)}), bf16[64,6,2048]{2,1,0:T(8,128)(2,1)}, u32[]{:S(2)}, u32[]{:S(2)}) async-start(bf16[64,6,2048]{2,1,0:T(8,128)(2,1)} %reshape.206), calls=%async_computation | async-start | bytes 4194304 | tf_op jit(solution)/shard_map/all_to_all | solution.py:87
  49.2 0.9 reduce-window.16
  51.2 1.8 multiply_convert_fusion
  52.9 3.7 reshape.211
  56.6 181.4 %all-to-all-done = bf16[64,6,2048]{2,1,0:T(8,128)(2,1)} async-done(((bf16[64,6,2048]{2,1,0:T(8,128)(2,1)}), bf16[64,6,2048]{2,1,0:T(8,128)(2,1)}, u32[]{:S(2)}, u32[]{:S(2)}) %all-to-all-start) | async-done | bytes 1572896 | tf_op jit(solution)/shard_map/all_to_all | solution.py:87
  238.0 13.1 %all-to-all-start.2 = ((bf16[64,6,2048]{2,1,0:T(8,128)(2,1)}), bf16[64,6,2048]{2,1,0:T(8,128)(2,1)}, u32[]{:S(2)}, u32[]{:S(2)}) async-start(bf16[64,6,2048]{2,1,0:T(8,128)(2,1)} %reshape.211), calls=%async_computation.2 | async-start | bytes 4194304 | tf_op jit(solution)/shard_map/all_to_all | solution.py:93
  251.1 3.7 reshape.207
  254.8 5.1 fusion.5
  259.9 6.8 fusion.7
  266.6 3.7 reshape.208
  270.3 170.7 %all-to-all-done.2 = bf16[64,6,2048]{2,1,0:T(8,128)(2,1)} async-done(((bf16[64,6,2048]{2,1,0:T(8,128)(2,1)}), bf16[64,6,2048]{2,1,0:T(8,128)(2,1)}, u32[]{:S(2)}, u32[]{:S(2)}) %all-to-all-start.2) | async-done | bytes 1572896 | tf_op jit(solution)/shard_map/all_to_all | solution.py:93
  441.0 13.1 %all-to-all-start.1 = ((bf16[64,6,2048]{2,1,0:T(8,128)(2,1)}), bf16[64,6,2048]{2,1,0:T(8,128)(2,1)}, u32[]{:S(2)}, u32[]{:S(2)}) async-start(bf16[64,6,2048]{2,1,0:T(8,128)(2,1)} %reshape.208), calls=%async_computation.1 | async-start | bytes 4194304 | tf_op jit(solution)/shard_map/all_to_all | solution.py:92
  454.3 3.7 reshape.212
  458.0 4.8 fusion
  462.8 4.6 copy.52
  467.8 306.3 %reduce-scatter.4.cloned.1.call-done = bf16[128,704]{1,0:T(8,128)(2,1)} async-done(((bf16[2048,704]{1,0:T(8,128)(2,1)}), bf16[128,704]{1,0:T(8,128)(2,1)}) %reduce-scatter.4.cloned.1.call-update) | async-done | bytes 180240
  774.1 1.1 copy.53
  776.0 3.7 reshape.209
  779.7 6.7 gather_fusion
  786.4 3.9 reshape.213
  790.3 4.5 multiply_reduce_fusion
  (56 shorter events, 7.3 us)
Async XLA Ops:
  7.2 252.7 %copy-start = (bf16[1,704,2048]{2,1,0:T(8,128)(2,1)S(1)}, bf16[1,704,2048]{2,1,0:T(8,128)(2,1)}, u32[]{:S(2)}) copy-start(bf16[1,704,2048]{2,1,0:T(8,128)(2,1)} %param.23) | copy-start | bytes 8650756
  18.4 29.7 %copy-start.4 = (s32[64]{0:T(128)S(1)}, s32[64]{0:T(128)}, u32[]{:S(2)}) copy-start(s32[64]{0:T(128)} %param.19) | copy-start | bytes 772
  18.4 30.1 %copy-start.2 = (s32[64,6]{0,1:T(8,128)S(1)}, s32[64,6]{0,1:T(8,128)}, u32[]{:S(2)}) copy-start(s32[64,6]{0,1:T(8,128)} %param.17) | copy-start | bytes 4612
  18.4 30.6 %copy-start.3 = (f32[64,6]{0,1:T(8,128)S(1)}, f32[64,6]{0,1:T(8,128)}, u32[]{:S(2)}) copy-start(f32[64,6]{0,1:T(8,128)} %param.18) | copy-start | bytes 4612
  18.4 32.7 %copy-start.1 = (bf16[64,2048]{1,0:T(8,128)(2,1)S(1)}, bf16[64,2048]{1,0:T(8,128)(2,1)}, u32[]{:S(2)}) copy-start(bf16[64,2048]{1,0:T(8,128)(2,1)} %param.16) | copy-start | bytes 786436
  18.4 219.6 %all-to-all-start = ((bf16[64,6,2048]{2,1,0:T(8,128)(2,1)}), bf16[64,6,2048]{2,1,0:T(8,128)(2,1)}, u32[]{:S(2)}, u32[]{:S(2)}) async-start(bf16[64,6,2048]{2,1,0:T(8,128)(2,1)} %reshape.206), calls=%async_computation | async-start | bytes 4194304 | tf_op jit(solution)/shard_map/all_to_all | solution.py:87
  238.0 202.9 %all-to-all-start.2 = ((bf16[64,6,2048]{2,1,0:T(8,128)(2,1)}), bf16[64,6,2048]{2,1,0:T(8,128)(2,1)}, u32[]{:S(2)}, u32[]{:S(2)}) async-start(bf16[64,6,2048]{2,1,0:T(8,128)(2,1)} %reshape.211), calls=%async_computation.2 | async-start | bytes 4194304 | tf_op jit(solution)/shard_map/all_to_all | solution.py:93
  441.0 335.0 %all-to-all-start.1 = ((bf16[64,6,2048]{2,1,0:T(8,128)(2,1)}), bf16[64,6,2048]{2,1,0:T(8,128)(2,1)}, u32[]{:S(2)}, u32[]{:S(2)}) async-start(bf16[64,6,2048]{2,1,0:T(8,128)(2,1)} %reshape.208), calls=%async_computation.1 | async-start | bytes 4194304 | tf_op jit(solution)/shard_map/all_to_all | solution.py:92
  454.0 320.1 %reduce-scatter.4.cloned.1.call-start = ((), (), s32[]{:S(2)}) async-start(), calls=%async_computation.4 | async-start | bytes 3342336
Sparse Core Ops, SparseCore 0:
  467.5 306.5 reduce-scatter.3
where the time goes:
time: 803 us; the launch traced here: 802 us
  waiting for transfers between devices  658 us (82%)
  starting transfers between devices  56 us (7%)
  local copies, waits for them, and re-layouts  42.9 us (5%)
  matrix products  21.2 us (3%)
  between operations  14.2 us (2%)
  other arithmetic  8.88 us (1%)
    unnamed x2, waiting for transfers between devices  306 us
    all_to_all x1, waiting for transfers between devices, body(): lax.all_to_all(a_send, 'expert', split_axis=0, concat_axis=0, tiled=True)  181 us
    all_to_all x1, waiting for transfers between devices, body(): lax.all_to_all(b_send, 'expert', split_axis=0, concat_axis=0, tiled=True)  171 us
    all_to_all x1, starting transfers between devices, body(): lax.all_to_all(a_send, 'expert', split_axis=0, concat_axis=0, tiled=True)  29.7 us
  transfers between devices with their start and end apart: 4, of which 3 were waited for; matrix products, arithmetic and copies ran while one was open for 5% of the time, Pallas kernels for 0%

commit v1 on v0

v1 whole, which is shorter than its diff:
```python
import functools
import jax
import jax.numpy as jnp
from jax import lax
from jax.experimental import pallas as pl
from jax.experimental.pallas import tpu as pltpu
from jax.sharding import PartitionSpec as P

MESH = pl.DeviceIdType.MESH
BF16, F32, I32 = jnp.bfloat16, jnp.float32, jnp.int32
NX, NY, NZ, NC = 4, 4, 2, 2
SLOT = 8
OFFSET = 8
CHUNKS = 2


def dot(lhs, rhs, left, right):
    return lax.dot_general(lhs, rhs, (((left,), (right,)), ((), ())), preferred_element_type=F32)


def iota(shape, dim):
    return lax.broadcasted_iota(I32, shape, dim)


def slot_table(ids, gates, valid, planes, capacity):
    top, tokens = ids.shape
    experts = planes * NX
    expert = iota((experts, tokens), 0)
    chosen = jnp.zeros((experts, tokens), F32)
    gate = jnp.zeros((experts, tokens), F32)
    for k in range(top):
        here = ids[k : k + 1, :] == expert
        chosen = jnp.where(here, 1.0, chosen)
        gate = jnp.where(here, gates[k : k + 1, :], gate)
    live = jnp.where(valid > 0, chosen, 0.0)
    earlier = (iota((tokens, tokens), 0) < iota((tokens, tokens), 1)).astype(F32).astype(BF16)
    position = dot(live.astype(BF16), earlier, 1, 0)
    position = jnp.where(live > 0, position, 127.0)
    token = (iota((experts, tokens), 1) + 1).astype(F32)
    lane = iota((experts, 128), 1)
    mine = lax.rem(iota((experts, 128), 0), NX) == lax.rem(lane // 16, 4)
    spread = jnp.zeros((experts, 128), F32)
    for c in range(capacity):
        here = position == float(c)
        who = jnp.sum(jnp.where(here, token, 0.0), axis=1, keepdims=True)
        weight = jnp.sum(jnp.where(here, gate, 0.0), axis=1, keepdims=True)
        at_c = mine & (lax.rem(lane, 16) == c)
        spread = jnp.where(at_c, jnp.where(lane < 64, who, weight), spread)
    plane_of = (iota((planes, experts), 1) // NX == iota((planes, experts), 0)).astype(F32)
    return lax.dot_general(
        plane_of, spread, (((1,), (0,)), ((), ())), precision=lax.Precision.HIGHEST, preferred_element_type=F32
    )


def pair_masks(row0, row1, tokens):
    row1 = pltpu.roll(row1, SLOT, 1)
    token = (iota((tokens, 128), 0) + 1).astype(F32)
    hit0, hit1 = token == row0, token == row1
    pick = jnp.concatenate([jnp.where(hit0, 1.0, 0.0), jnp.where(hit1, 1.0, 0.0)], axis=0)[:, :64]
    gate0, gate1 = pltpu.roll(row0, 64, 1), pltpu.roll(row1, 64, 1)
    gate = jnp.concatenate([jnp.where(hit0, gate0, 0.0), jnp.where(hit1, gate1, 0.0)], axis=0)[:, :64]
    return pick, gate


def split(value):
    high = value.astype(BF16)
    return high, (value - high.astype(F32)).astype(BF16)


def kernel(
    ZL,
    a_tok, a_ids, a_gates, a_valid, b_cot, b_ids, b_gates, b_valid, b_hid, w_gate, w_up, w_down,
    out_a, out_g,
    agA, tabA, agB, tabB, stA, stB, xA, xB, hid, yo, yb, lsend, lrecv, rsend, rrecv,
    wg, wu, wd, hT, hP, part, crecv, csum, yr1, yr2, zs, zr, own,
    local, sA, rA, stabA, rtabA, sB, rB, stabB, rtabB, sxA, rxA, sxB, rxB, sy, ry, sR, rR, sC, rC, sY1, rY1, sY2, rY2, sZ, rZ,
):
    NP = ZL // 2
    T, D = a_tok.shape
    F = w_down.shape[1]
    NB = NZ * NY
    capacity = b_hid.shape[2] // (ZL * NX)
    ring = ZL * NZ
    e, r = lax.axis_index("expert"), lax.axis_index("replica")
    z, x = e // NX, lax.rem(e, NX)
    zh, y, c = r // (NY * NC), lax.rem(r // NC, NY), lax.rem(r, NC)
    place = zh * ZL + z

    def device(place_, x_, y_, c_):
        place_ = lax.rem(place_ + ring, ring)
        return (lax.rem(place_, ZL) * NX + x_, (place_ // ZL * NY + y_) * NC + c_)

    up, down = device(place + 1, x, y, c), device(place - 1, x, y, c)
    side = [None] + [device(place, lax.rem(x + d, NX), y, c) for d in range(1, NX)]
    partner = device(place, x, y, 1 - c)
    y_up, y_down = device(place, x, lax.rem(y + 1, NY), c), device(place, x, lax.rem(y + NY - 1, NY), c)
    far = device(place + ZL, x, y, c)

    def send(src, dst, s, r_, to):
        return pltpu.make_async_remote_copy(
            src_ref=src, dst_ref=dst, send_sem=s, recv_sem=r_, device_id=to, device_id_type=MESH
        )

    rows = T // CHUNKS

    def part_rows(k):
        return pl.ds(k * rows, rows)

    loads = [
        pltpu.make_async_copy(a_tok, agA.at[0, 1], local.at[0]),
        pltpu.make_async_copy(b_cot, agB.at[z], local.at[1]),
        pltpu.make_async_copy(b_hid.at[0], hT, local.at[2]),
        pltpu.make_async_copy(w_gate.at[0], wg, local.at[3]),
        pltpu.make_async_copy(w_up.at[0], wu, local.at[4]),
        pltpu.make_async_copy(w_down.at[0], wd, local.at[5]),
    ]
    for load in loads:
        load.start()

    barrier = pltpu.get_barrier_semaphore()
    peers = [up, down, *side[1:], partner, y_up, y_down, far]
    for peer in peers:
        pl.semaphore_signal(barrier, inc=1, device_id=peer, device_id_type=MESH)
    pl.semaphore_wait(barrier, len(peers))

    def a_up(n, k):
        return send(agA.at[n, 0, part_rows(k)], agA.at[n + 1, 0, part_rows(k)], sA.at[0, n + 1, k], rA.at[0, n + 1, k], up)

    def a_up_first(k):
        return send(agA.at[0, 1, part_rows(k)], agA.at[0, 0, part_rows(k)], sA.at[0, 0, k], rA.at[0, 0, k], up)

    def a_down(n, k):
        return send(agA.at[n, 1, part_rows(k)], agA.at[n + 1, 1, part_rows(k)], sA.at[1, n + 1, k], rA.at[1, n + 1, k], down)

    def ta_up(n):
        return send(tabA.at[n, 0], tabA.at[n + 1, 0], stabA.at[0, n + 1], rtabA.at[0, n + 1], up)

    def ta_up_first():
        return send(tabA.at[0, 1], tabA.at[0, 0], stabA.at[0, 0], rtabA.at[0, 0], up)

    def ta_down(n):
        return send(tabA.at[n, 1], tabA.at[n + 1, 1], stabA.at[1, n + 1], rtabA.at[1, n + 1], down)

    def b_send(way, s, k):
        return send(agB.at[s, part_rows(k)], agB.at[s, part_rows(k)], sB.at[way, s, k], rB.at[s, k], (up, down)[way])

    def tb_send(way, s):
        return send(tabB.at[s], tabB.at[s], stabB.at[way, s], rtabB.at[s], (up, down)[way])

    def x_send(stage, arrived, ss, rr, n, d):
        return send(stage.at[n, lax.rem(x + d, NX)], arrived.at[n, x], ss.at[n, d - 1], rr.at[n, d - 1], side[d])

    def x_wait(stage, arrived, ss, rr, n, d):
        return send(stage.at[n, x], arrived.at[n, lax.rem(x + NX - d, NX)], ss.at[n, d - 1], rr.at[n, d - 1], side[d])

    loads[1].wait()
    for k in range(CHUNKS):
        @pl.when(z < ZL - 1)
        def _():
            b_send(0, z, k).start()

        @pl.when(z > 0)
        def _():
            b_send(1, z, k).start()

    loads[0].wait()
    if OFFSET == 0:
        for k in range(CHUNKS):
            a_up_first(k).start()
            a_down(0, k).start()
    tabB[z] = slot_table(b_ids[...], b_gates[...], b_valid[...], ZL, capacity)

    @pl.when(z < ZL - 1)
    def _():
        tb_send(0, z).start()

    @pl.when(z > 0)
    def _():
        tb_send(1, z).start()

    tabA[0, 1] = slot_table(a_ids[...], a_gates[...], a_valid[...], ZL, capacity)
    if OFFSET == 0:
        ta_up_first().start()
        ta_down(0).start()

    loads[2].wait()
    wide = NP * NX * 2 * SLOT
    col = iota((1, wide), 1)
    slot = lax.rem(col, SLOT)
    source = (2 * (col // (NX * 2 * SLOT)) + lax.rem(col // SLOT, 2)) * NX + lax.rem(col // (2 * SLOT), NX)
    column = jnp.where(slot < capacity, source * capacity + slot, -1)
    mover = (iota((hT.shape[1], wide), 0) == column).astype(F32).astype(BF16)
    hP[...] = dot(hT[...], mover, 1, 0).astype(BF16)
    for load in loads[3:]:
        load.wait()

    tile = min(512, D)

    def columns(n):
        return pl.ds(pl.multiple_of(n * tile, tile), tile)

    def pick_a(n):
        pick, _ = pair_masks(tabA[n, 0, pl.ds(z, 1), :], tabA[n, 1, pl.ds(z, 1), :], T)
        pick = pick.astype(BF16)

        def one(q, _):
            block = agA[n, :, :, columns(q)].reshape(2 * T, tile)
            stA[n, :, :, columns(q)] = dot(pick, block, 0, 0).astype(BF16).reshape(NX, 2 * SLOT, tile)
            return 0

        lax.fori_loop(0, D // tile, one, 0)
        for d in range(1, NX):
            x_send(stA, xA, sxA, rxA, n, d).start()
        xA[n, x] = stA[n, x]

    def pick_b(m):
        _, gate = pair_masks(tabB[2 * m, pl.ds(z, 1), :], tabB[2 * m + 1, pl.ds(z, 1), :], T)
        high, low = split(gate)

        def one(q, _):
            block = agB[pl.ds(2 * m, 2), :, columns(q)].reshape(2 * T, tile)
            rows_ = dot(high, block, 0, 0) + dot(low, block, 0, 0)
            stB[m, :, :, columns(q)] = rows_.astype(BF16).reshape(NX, 2 * SLOT, tile)
            return 0

        lax.fori_loop(0, D // tile, one, 0)
        for d in range(1, NX):
            x_send(stB, xB, sxB, rxB, m, d).start()
        xB[m, x] = stB[m, x]

    f_tiles = [(f, min(256, F - f)) for f in range(0, F, 256)]

    def experts(n, count):
        for q in range(count):
            for d in range(1, NX):
                x_wait(stA, xA, sxA, rxA, n + q, d).wait_recv()
        size = count * NX * 2 * SLOT
        inputs = xA[pl.ds(n, count)].reshape(size, D)
        for f, width in f_tiles:
            gate = dot(inputs, wg[f : f + width, :], 1, 1)
            lift = dot(inputs, wu[f : f + width, :], 1, 1)
            hid[:, f : f + width] = (gate / (1.0 + jnp.exp(-gate)) * lift).astype(BF16)

        def one(q, _):
            result = dot(hid[...], wd[:, columns(q)], 1, 0).astype(BF16)
            yo[pl.ds(n, count), :, :, columns(q)] = result.reshape(count, NX, 2 * SLOT, tile)
            return 0

        lax.fori_loop(0, D // tile, one, 0)
        for q in reversed(range(count)):
            for d in range(1, NX):
                x_send(yo, yb, sy, ry, n + q, d).start()
            yb[n + q, x] = yo[n + q, x]

    half = D // 2
    sub = min(512, half)

    def l_send(n, h):
        return send(lsend.at[n, h], lrecv.at[n, h], sR.at[0, n, h], rR.at[0, n, h], down)

    def r_send(n, h):
        return send(rsend.at[n, h], rrecv.at[n, h], sR.at[1, n, h], rR.at[1, n, h], up)

    def combine(n, first, last):
        for d in range(1, NX):
            x_wait(yo, yb, sy, ry, n, d).wait_recv()
        _, gate = pair_masks(tabA[n, 0, pl.ds(z, 1), :], tabA[n, 1, pl.ds(z, 1), :], T)
        high, low = split(gate)
        for h in range(2):
            sums = []
            for q in range(half // sub):
                block = yb[n, :, :, h * half + q * sub : h * half + (q + 1) * sub].reshape(NX * 2 * SLOT, sub)
                sums.append(dot(high, block, 1, 0) + dot(low, block, 1, 0))
            if not first:
                l_send(n + 1, h).wait_recv()
            for q, value in enumerate(sums):
                at = slice(q * sub, (q + 1) * sub)
                total = value[:T]
                if not first:
                    total = total + lrecv[n + 1, h, :, at].astype(F32)
                lsend[n, h, :, at] = total.astype(BF16)
            l_send(n, h).start()
            if not first:
                r_send(n + 1, h).wait_recv()
            if last:
                l_send(n, h).wait_recv()
            for q, value in enumerate(sums):
                at = slice(q * sub, (q + 1) * sub)
                total = value[T:]
                if not first:
                    total = total + rrecv[n + 1, h, :, at].astype(F32)
                if last:
                    total = total + lrecv[n, h, :, at].astype(F32)
                    out_a[:, h * half + q * sub : h * half + (q + 1) * sub] = total.astype(BF16)
                else:
                    rsend[n, h, :, at] = total.astype(BF16)
            if not last:
                r_send(n, h).start()

    turns = [(h, d) for h in range(2) for d in (2, 1, NY - 1, 0)]

    def block_of(h, d):
        half_of = (1 - zh) if h == 0 else zh
        return half_of * NY + lax.rem(y + d, NY)

    def core_send(b):
        return send(part.at[b, 1 - c], crecv.at[b], sC.at[b], rC.at[b], partner)

    FH = F // 2

    def y1_send(h, way):
        at = pl.ds(way * FH, FH)
        return send(csum.at[block_of(h, 2), at], yr1.at[h, way], sY1.at[h, way], rY1.at[h, way], (y_up, y_down)[way])

    def y2_send(h, way):
        return send(csum.at[block_of(h, (1, NY - 1)[way])], yr2.at[h, way], sY2.at[h, way], rY2.at[h, way], (y_up, y_down)[way])

    def z_send():
        return send(zs, zr, sZ, rZ, far)

    def gradient_blocks():
        for n in range(NP):
            for d in range(1, NX):
                x_wait(stB, xB, sxB, rxB, n, d).wait_recv()
        for h, d in turns:
            b = block_of(h, d)
            cot = xB[:, :, :, pl.ds(pl.multiple_of(b * 256, 256), 256)].reshape(wide, 256)
            value = dot(hP[...], cot, 1, 0)
            part[b, 0] = value[:, :128].astype(BF16)
            part[b, 1] = value[:, 128:].astype(BF16)
            core_send(b).start()

    def core_sums(h):
        for d in (2, 1, NY - 1, 0):
            b = block_of(h, d)
            core_send(b).wait_recv()
            csum[b] = (part[b, c].astype(F32) + crecv[b].astype(F32)).astype(BF16)
            if d == 2:
                for way in range(2):
                    y1_send(h, way).start()

    def y_sums(h):
        for way in range(2):
            b = block_of(h, (1, NY - 1)[way])
            at = pl.ds(way * FH, FH)
            y1_send(h, way).wait_recv()
            csum[b, at] = (csum[b, at].astype(F32) + yr1[h, way].astype(F32)).astype(BF16)
            y2_send(h, way).start()

    def y_last(h):
        for way in range(2):
            y2_send(h, way).wait_recv()
        total = csum[block_of(h, 0)].astype(F32) + yr2[h, 0].astype(F32) + yr2[h, 1].astype(F32)
        if h == 0:
            zs[...] = total.astype(BF16)
            z_send().start()
        else:
            own[...] = total

    B_LAST = ZL - 1
    A_END = OFFSET + 2 * NP + 1

    def step(j, _):
        i = j - OFFSET
        for k in range(CHUNKS):
            @pl.when((j <= B_LAST) & (z - j >= 0))
            def _():
                b_send(0, z - j, k).wait_recv()

                @pl.when(z < ZL - 1)
                def _():
                    b_send(0, z - j, k).start()

            @pl.when((j <= B_LAST) & (z + j < ZL))
            def _():
                b_send(1, z + j, k).wait_recv()

                @pl.when(z > 0)
                def _():
                    b_send(1, z + j, k).start()

            if OFFSET > 0:
                @pl.when(i == 0)
                def _():
                    a_up_first(k).start()
                    a_down(0, k).start()

            @pl.when((i >= 1) & (i <= NP))
            def _():
                send(agA.at[i - 1, 0, part_rows(k)], agA.at[i - 1, 0, part_rows(k)], sA.at[0, i - 1, k], rA.at[0, i - 1, k], up).wait_recv()

                @pl.when(i < NP)
                def _():
                    a_up(i - 1, k).start()
                    a_down(i - 1, k).wait_recv()

                @pl.when(i < NP - 1)
                def _():
                    a_down(i, k).start()

        @pl.when((j <= B_LAST) & (z - j >= 0))
        def _():
            tb_send(0, z - j).wait_recv()

            @pl.when(z < ZL - 1)
            def _():
                tb_send(0, z - j).start()

        @pl.when((j <= B_LAST) & (z + j < ZL))
        def _():
            tb_send(1, z + j).wait_recv()

            @pl.when(z > 0)
            def _():
                tb_send(1, z + j).start()

        if OFFSET > 0:
            @pl.when(i == 0)
            def _():
                ta_up_first().start()
                ta_down(0).start()

        @pl.when((i >= 1) & (i <= NP))
        def _():
            send(tabA.at[i - 1, 0], tabA.at[i - 1, 0], stabA.at[0, i - 1], rtabA.at[0, i - 1], up).wait_recv()

            @pl.when(i < NP)
            def _():
                ta_up(i - 1).start()
                ta_down(i - 1).wait_recv()

            @pl.when(i < NP - 1)
            def _():
                ta_down(i).start()

        even = 1 - lax.rem(z + j, 2)
        whole = even * ((z - j + 2 * ZL) // 2 - ZL) + (1 - even) * ((z + j - 1) // 2)

        @pl.when((j <= B_LAST) & (whole >= 0) & (whole < NP))
        def _():
            pick_b(whole)

        @pl.when((i >= 1) & (i <= NP))
        def _():
            pick_a(i - 1)

        @pl.when((i >= 3) & (i <= NP + 1) & (lax.rem(i + 2, 2) == 1))
        def _():
            experts(i - 3, 2)

        @pl.when(i == NP + 2)
        def _():
            combine(NP - 1, True, False)

        @pl.when((i > NP + 2) & (i < 2 * NP + 1))
        def _():
            combine(2 * NP + 1 - i, False, False)

        @pl.when(j == B_LAST + 1)
        def _():
            gradient_blocks()

        @pl.when(j == B_LAST + 2)
        def _():
            core_sums(0)
            core_sums(1)

        @pl.when(j == B_LAST + 3)
        def _():
            y_sums(0)
            y_sums(1)

        @pl.when(j == B_LAST + 4)
        def _():
            y_last(0)
            y_last(1)

        return 0

    lax.fori_loop(1, max(A_END, B_LAST + 5), step, 0)
    combine(0, NP == 1, True)
    z_send().wait_recv()
    out_g[0] = own[...] + zr[...].astype(F32)

    for k in range(CHUNKS):
        a_up_first(k).wait_send()
    ta_up_first().wait_send()

    def done_a(n, _):
        for k in range(CHUNKS):
            a_up(n, k).wait_send()
        ta_up(n).wait_send()
        return 0

    lax.fori_loop(0, NP - 1, done_a, 0)

    def done_down(n, _):
        for k in range(CHUNKS):
            a_down(n, k).wait_send()
        ta_down(n).wait_send()
        return 0

    lax.fori_loop(0, NP - 1, done_down, 0)

    def done_b(s, _):
        @pl.when((s <= z) & (z < ZL - 1))
        def _():
            for k in range(CHUNKS):
                b_send(0, s, k).wait_send()
            tb_send(0, s).wait_send()

        @pl.when((s >= z) & (z > 0))
        def _():
            for k in range(CHUNKS):
                b_send(1, s, k).wait_send()
            tb_send(1, s).wait_send()

        return 0

    lax.fori_loop(0, ZL, done_b, 0)

    def done_pairs(n, _):
        for d in range(1, NX):
            x_send(stA, xA, sxA, rxA, n, d).wait_send()
            x_send(stB, xB, sxB, rxB, n, d).wait_send()
            x_send(yo, yb, sy, ry, n, d).wait_send()
        for h in range(2):
            l_send(n, h).wait_send()

            @pl.when(n > 0)
            def _():
                r_send(n, h).wait_send()

        return 0

    lax.fori_loop(0, NP, done_pairs, 0)

    def done_blocks(b, _):
        core_send(b).wait_send()
        return 0

    lax.fori_loop(0, NB, done_blocks, 0)
    for h in range(2):
        for way in range(2):
            y1_send(h, way).wait_send()
            y2_send(h, way).wait_send()
    z_send().wait_send()


def body(a_tokens, a_ids, a_gates, a_valid, b_cot, b_ids, b_gates, b_valid, b_hidden, w_gate, w_up, w_down):
    ZL = lax.axis_size("expert") // NX
    NP = ZL // 2
    T, D = a_tokens.shape
    F = w_down.shape[1]
    NB = NZ * NY
    wide = NP * NX * 2 * SLOT
    whole, vmem, dma = pl.BlockSpec(memory_space=pl.ANY), pl.BlockSpec(memory_space=pltpu.VMEM), pltpu.SemaphoreType.DMA
    tab = lambda *lead: pltpu.VMEM((*lead, ZL, 128), F32)
    slots = pltpu.VMEM((NP, NX, 2 * SLOT, D), BF16)
    moving = pltpu.VMEM((NP, 2, T, D // 2), BF16)
    scratch = [
        pltpu.VMEM((NP, 2, T, D), BF16), tab(NP, 2), pltpu.VMEM((ZL, T, D), BF16), tab(ZL),
        slots, slots, slots, slots, pltpu.VMEM((2 * NX * 2 * SLOT, F), BF16), slots, slots,
        moving, moving, moving, moving,
        pltpu.VMEM((F, D), BF16), pltpu.VMEM((F, D), BF16), pltpu.VMEM((F, D), BF16),
        pltpu.VMEM((F, b_hidden.shape[1]), BF16), pltpu.VMEM((F, wide), BF16),
        pltpu.VMEM((NB, NC, F, 128), BF16), pltpu.VMEM((NB, F, 128), BF16), pltpu.VMEM((NB, F, 128), BF16),
        pltpu.VMEM((2, 2, F // 2, 128), BF16), pltpu.VMEM((2, 2, F, 128), BF16),
        pltpu.VMEM((F, 128), BF16), pltpu.VMEM((F, 128), BF16), pltpu.VMEM((F, 128), F32),
        dma((6,)),
        dma((2, NP, CHUNKS)), dma((2, NP, CHUNKS)), dma((2, NP)), dma((2, NP)),
        dma((2, ZL, CHUNKS)), dma((ZL, CHUNKS)), dma((2, ZL)), dma((ZL,)),
        dma((NP, NX - 1)), dma((NP, NX - 1)), dma((NP, NX - 1)), dma((NP, NX - 1)), dma((NP, NX - 1)), dma((NP, NX - 1)),
        dma((2, NP, 2)), dma((2, NP, 2)), dma((NB,)), dma((NB,)),
        dma((2, 2)), dma((2, 2)), dma((2, 2)), dma((2, 2)), dma, dma,
    ]
    return pl.pallas_call(
        functools.partial(kernel, ZL),
        out_shape=(jax.ShapeDtypeStruct((T, D), BF16), jax.ShapeDtypeStruct((1, F, 128), F32)),
        in_specs=[whole, vmem, vmem, vmem, whole, vmem, vmem, vmem, whole, whole, whole, whole],
        out_specs=(vmem, vmem),
        scratch_shapes=scratch,
        compiler_params=pltpu.CompilerParams(
            collective_id=0, has_side_effects=True, vmem_limit_bytes=67_043_328
        ),
    )(
        a_tokens, a_ids.T, a_gates.T, a_valid[None], b_cot, b_ids.T, b_gates.T, b_valid[None],
        jnp.swapaxes(b_hidden, 1, 2), jnp.swapaxes(w_gate, 1, 2), jnp.swapaxes(w_up, 1, 2), w_down,
    )


def solution(mesh):
    tokens, flat = P(("expert", "replica"), None), P(("expert", "replica"))
    weight = P("expert", None, None)
    return jax.shard_map(
        body,
        mesh=mesh,
        in_specs=(
            tokens, tokens, tokens, flat, tokens, tokens, tokens, flat, P("expert", "replica", None), weight, weight, weight,
        ),
        out_specs=(tokens, P("expert", None, "replica")),
        check_vma=False,
    )
```

time: 803 us -> 260 us (0.32)
  the two profiles are of different devices: /device:TPU:2 before, /device:TPU:8 now
where the time goes in v1:
time: 260 us; the launch traced here: 259 us
  Pallas kernels  255 us (98%)
  local copies, waits for them, and re-layouts  3.41 us (1%)
    pallas_call x1, Pallas kernels, body(): pl.pallas_call(functools.partial(kernel, ZL), out_shape=(jax.ShapeDtypeSt...  255 us

profile of v1, /device:TPU:8, one launch (start us, length us, event | category | flops | bytes accessed | tf_op | source)
XLA Modules:
  0.0 259.5 jit_solution(17999497774954586257)
XLA Ops:
  0.6 255.4 %shard_map.131 = (bf16[64,2048]{1,0:T(8,128)(2,1)}, f32[1,704,128]{2,1,0:T(8,128)}) custom-call(bf16[64,2048]{1,0:T(8,128)(2,1)} %a_tok.1, s32[6,64]{1,0:T(8,128)} %bitcast.12, f32[6,64]{1,0:T(8,128)} %bitcast.13, s32[1,64]{1,0:T(1,128)} %bitcast.16, bf16[64,2048]{1,0:T(8,128)(2,1)} %b_cot.1, s32[6,64]{1,0:T(8,128)} %bitcast.14, f32[6,64]{1,0:T(8,128)} %bitcast.15, ...), custom_call_target="tpu_custom_call" | custom-call | tf_op jit(solution)/shard_map/pallas_call | solution.py:577
  256.0 1.7 copy.16
  257.7 1.7 copy.17
